TPU v7x, 256 devices: a whole 4x4x8 slice. The times are simulated.
256 devices in a mesh: grid: 32 (over y, x, core), rows: 8 (over z).
Axes of the slice: x: 4, y: 4, z: 8, core: 2. Of those that a mesh axis runs over, the one named last changes fastest.
Arguments:
- density: bfloat16 [32, 128, 4096], P(None, 'rows', 'grid'), as said below
- basis_values: bfloat16 [64, 16, 128, 512], P('grid', None, 'rows'), may hold values from -0.59765625 to 0.59765625
- grid_points: float32 [64, 3, 512], P('grid'), may hold values from -4 to 4
- grid_weights: float32 [64, 512], P('grid'), may hold values from 0.05 to 1
- screened_blocks: int32 [64, 16], P('grid'), may hold values from 0 to 31, as said below
Outputs:
- exchange: float32 [32, 128, 4096], P(None, 'rows', 'grid')
Inputs may be any that keep to these rules, and one draw needn't show every extreme that they name: density is symmetric: density[a, i, b * 128 + j] equals density[b, j, a * 128 + i]. `screened_blocks`: each row holds 16 distinct block numbers.
All inputs are finite; a program needn't handle non-finite values.
Results may differ from a plain program's by a relative error of at most 0.00055.
The roundings to bfloat16 on the way count: a program that leaves them out, or rounds other values in their place, can miss the bound.
Values may be sent and summed in bfloat16 or wider, within the bound.
A program may use at most 64 MiB of HBM per device.

v0:
```python
import jax
import jax.numpy as jnp
from jax import lax
from jax.sharding import PartitionSpec as P


def copy_for_each(shard, axis):
    copies = jnp.broadcast_to(shard, (lax.axis_size(axis), *shard.shape))
    return lax.all_to_all(copies, axis, split_axis=0, concat_axis=0, tiled=True)


def joined_along(blocks, dim):
    shape = list(blocks.shape[1:])
    shape[dim] *= blocks.shape[0]
    return jnp.moveaxis(blocks, 0, dim).reshape(shape)


def gather_directly(shard, axis, dim):
    blocks = copy_for_each(shard, axis)
    return joined_along(blocks, dim)


def body(density, basis_values, grid_points, grid_weights, screened_blocks):
    nblocks = density.shape[0]
    rows_mine = density.shape[1]
    block_size = rows_mine * lax.axis_size("rows")
    nbasis = nblocks * block_size
    nsig = basis_values.shape[1]
    npoints = basis_values.shape[3]
    stripe = lax.all_gather(density, "grid", axis=2, tiled=True)
    totals = jnp.zeros((nblocks, rows_mine, nblocks, block_size), jnp.float32)
    for batch_index in range(basis_values.shape[0]):
        blocks = screened_blocks[batch_index]
        row_pick = jnp.take(stripe, blocks, axis=0).reshape(nsig * rows_mine, nblocks, block_size)
        chosen = jnp.take(row_pick, blocks, axis=1)
        local_values = basis_values[batch_index]
        x_mine = local_values.reshape(nsig * rows_mine, npoints)
        fsum = jnp.einsum(
            "mtk,tkp->mp",
            chosen,
            gather_directly(local_values, "rows", 1),
            preferred_element_type=jnp.float32,
        )
        fmat = fsum.astype(jnp.bfloat16)
        intersection_part = lax.dot_general(
            x_mine, fmat, (((0,), (0,)), ((), ())), preferred_element_type=jnp.float32
        )
        intersection = lax.psum(intersection_part, "rows")
        places = grid_points[batch_index]
        weights = grid_weights[batch_index]
        diffs = places[:, :, None] - places[:, None, :]
        kern = 1.0 / jnp.sqrt(jnp.sum(diffs * diffs, axis=0) + 0.5)
        mixed = (weights[:, None] * kern * intersection).astype(jnp.bfloat16)
        potential = (
            jnp.dot(x_mine, mixed, preferred_element_type=jnp.float32) * weights[None, :]
        ).astype(jnp.bfloat16)
        potential = potential.reshape(nsig, rows_mine, npoints)
        block_k = jnp.einsum(
            "mp,tkp->mtk",
            x_mine,
            lax.all_gather(potential, "rows", axis=1, tiled=True),
            preferred_element_type=jnp.float32,
        )
        block_k = block_k.reshape(nsig, rows_mine, nsig, block_size)
        totals = totals.at[blocks[:, None], :, blocks[None, :], :].add(
            block_k.transpose(0, 2, 1, 3)
        )
    return lax.psum_scatter(
        totals.reshape(nblocks, rows_mine, nbasis), "grid", scatter_dimension=2, tiled=True
    )


def solution(mesh):
    placed = (
        P(None, "rows", "grid"),
        P("grid", None, "rows", None),
        P("grid", None, None),
        P("grid", None),
        P("grid", None),
    )
    return jax.shard_map(
        body, mesh=mesh, in_specs=placed, out_specs=P(None, "rows", "grid"), check_vma=False
    )
```

profile of v0, /device:TPU:2, one launch (start us, length us, event | category | flops | bytes accessed | tf_op | source)
XLA Modules:
  0.0 494.6 jit_solution(1196830963108560420)
XLA Ops:
  6.5 0.0 all-gather.4.cloned.1.call-start
  6.5 0.7 all-gather.4.cloned.1.call-update
  7.3 1.1 slice_bitcast_fusion
  8.4 0.3 broadcast_in_dim.59
  8.6 59.6 %all_to_all.10 = bf16[8,16,16,512]{3,2,1,0:T(8,128)(2,1)} all-to-all(bf16[8,16,16,512]{3,2,1,0:T(8,128)(2,1)S(1)} %broadcast_in_dim.59), channel_id=1, replica_groups=mesh['grid'=32,'rows'=8] {'rows'}, dimensions={0} | all-to-all | bytes 4194304 | tf_op jit(solution)/shard_map/all_to_all | solution.py:9
  68.2 1.6 broadcast_in_dim.55
  69.8 0.0 copy-start.3
  69.8 3.7 all-to-all-start
  73.5 0.0 all-reduce.3.cloned.1.call-start
  73.6 0.0 copy-done.3
  73.7 3.2 copy.34
  76.8 46.5 %all-to-all-done = bf16[8,16,16,512]{3,2,1,0:T(8,128)(2,1)S(1)} async-done(((bf16[8,16,16,512]{3,2,1,0:T(8,128)(2,1)}), bf16[8,16,16,512]{3,2,1,0:T(8,128)(2,1)S(1)}, u32[]{:S(2)}, u32[]{:S(2)}) %all-to-all-start) | async-done | bytes 2097184 | tf_op jit(solution)/shard_map/all_to_all | solution.py:9
  123.3 1.6 copy.29
  124.9 0.0 all-gather.4.cloned.1.call-done
  124.9 2.9 gather_fusion.2
  127.8 0.3 broadcast_select_fusion
  128.0 0.5 copy.42
  128.5 0.8 copy.33
  129.3 1.7 gather_fusion.3
  131.1 2.9 gather_fusion
  134.0 0.3 broadcast_select_fusion.1
  134.2 0.5 copy.41
  134.7 0.8 copy.28
  135.5 1.7 gather_fusion.1
  137.2 0.0 copy-start
  137.2 4.1 convolution_bitcast_fusion.2
  141.3 0.0 copy-done
  141.3 3.3 convolution_bitcast_fusion.3
  144.6 0.0 copy-start.1
  144.6 0.0 all-reduce.3.cloned.1.call-update
  144.6 0.0 copy-start.2
  144.6 0.0 all-gather.6.cloned.1.call-start
  144.6 0.6 copy-done.1
  145.3 0.4 multiply_reduce_fusion.1
  145.7 0.3 copy.27
  146.0 0.0 copy-done.2
  146.0 77.3 %all-reduce.3.cloned.1.call-done = (f32[512,512]{0,1:T(8,128)}, f32[512,512]{0,1:T(8,128)}) async-done(((f32[512,512]{0,1:T(8,128)}, f32[512,512]{0,1:T(8,128)}), (f32[512,512]{0,1:T(8,128)}, f32[512,512]{0,1:T(8,128)})) %all-reduce.3.cloned.1.call-update) | async-done | bytes 2097168 | tf_op jit(solution)/shard_map/psum | solution.py:48
  223.3 2.3 fusion
  225.6 0.0 all-gather.6.cloned.1.call-update
  225.7 0.0 all-gather.8.cloned.1.call-start
  225.7 0.4 multiply_reduce_fusion
  226.1 0.3 copy.32
  226.4 2.3 fusion.1
  228.7 0.0 all-gather.8.cloned.1.call-update
  228.7 0.2 reduce-scatter.2.cloned.1.call-start
  229.0 0.1 or_select_fusion
  229.1 0.1 reshape.140
  229.2 0.1 reshape.146
  229.3 36.4 %all-gather.6.cloned.1.call-done = bf16[16,128,512]{2,1,0:T(8,128)(2,1)} async-done(((bf16[16,16,512]{2,1,0:T(8,128)(2,1)}), bf16[16,128,512]{2,1,0:T(8,128)(2,1)}) %all-gather.6.cloned.1.call-update) | async-done | bytes 2097168 | tf_op jit(solution)/shard_map/all_gather | solution.py:61
  265.7 2.3 convolution_bitcast_fusion.1
  268.0 2.0 copy.30
  270.0 2.3 copy.31
  272.2 34.5 %all-gather.8.cloned.1.call-done = bf16[16,128,512]{2,1,0:T(8,128)(2,1)} async-done(((bf16[16,16,512]{2,1,0:T(8,128)(2,1)}), bf16[16,128,512]{2,1,0:T(8,128)(2,1)}) %all-gather.8.cloned.1.call-update) | async-done | bytes 2097168 | tf_op jit(solution)/shard_map/all_gather | solution.py:61
  306.8 3.6 convolution_bitcast_fusion
  310.4 3.1 copy.35
  313.5 3.6 copy.36
  317.1 4.2 broadcast_in_dim.51
  321.3 28.4 %scatter_fusion = f32[32,16,32,128]{3,1,2,0:T(8,128)} fusion(f32[32,16,32,128]{3,1,2,0:T(8,128)} %broadcast_in_dim.51, s32[256]{0:T(256)S(1)} %reshape.140, f32[256,16,128]{2,1,0:T(8,128)S(1)} %bitcast.107), kind=kCustom, calls=%fused_computation.4 | custom fusion | flops 524288 | bytes 6293504 | tf_op jit(solution)/shard_map/scatter-add | solution.py:65
  349.7 31.8 %scatter_fusion.1 = f32[32,16,32,128]{3,1,2,0:T(8,128)} fusion(f32[32,16,32,128]{3,1,2,0:T(8,128)} %scatter_fusion, s32[256]{0:T(256)S(1)} %reshape.146, f32[256,16,128]{2,1,0:T(8,128)} %bitcast.108), kind=kCustom, calls=%fused_computation.5 | custom fusion | flops 524288 | bytes 6293504 | tf_op jit(solution)/shard_map/scatter-add | solution.py:65
  381.5 7.8 %copy_bitcast_fusion = f32[32,16,4096]{2,1,0:T(8,128)} fusion(f32[32,16,32,128]{3,1,2,0:T(8,128)} %scatter_fusion.1), kind=kLoop, calls=%fused_computation.6 | loop fusion | bytes 16777216 | tf_op jit(solution)/shard_map/reshape | solution.py:69
  389.2 0.0 reduce-scatter.2.cloned.1.call-update
  389.3 98.8 %reduce-scatter.2.cloned.1.call-done = f32[32,16,128]{2,1,0:T(8,128)} async-done(((f32[32,16,4096]{2,1,0:T(8,128)}), f32[32,16,128]{2,1,0:T(8,128)}) %reduce-scatter.2.cloned.1.call-update) | async-done | bytes 262160 | tf_op jit(solution)/shard_map/reduce_scatter | solution.py:68
  (11 shorter events, 0.1 us)
Async XLA Ops:
  6.5 118.4 %all-gather.4.cloned.1.call-start = ((), (), s32[]{:S(2)}) async-start(), calls=%async_computation.3 | async-start | bytes 4325376 | tf_op jit(solution)/shard_map/all_gather | solution.py:30
  69.8 3.8 copy-start.3
  69.8 53.5 %all-to-all-start = ((bf16[8,16,16,512]{3,2,1,0:T(8,128)(2,1)}), bf16[8,16,16,512]{3,2,1,0:T(8,128)(2,1)S(1)}, u32[]{:S(2)}, u32[]{:S(2)}) async-start(bf16[8,16,16,512]{3,2,1,0:T(8,128)(2,1)} %broadcast_in_dim.55), calls=%async_computation | async-start | bytes 4194304 | tf_op jit(solution)/shard_map/all_to_all | solution.py:9
  73.5 149.8 %all-reduce.3.cloned.1.call-start = ((), (), s32[]{:S(2)}) async-start(), calls=%async_computation.7 | async-start | bytes 4194304 | tf_op jit(solution)/shard_map/psum | solution.py:48
  137.2 4.1 copy-start
  144.6 0.7 copy-start.1
  144.6 1.4 copy-start.2
  144.6 121.1 %all-gather.6.cloned.1.call-start = ((), (), s32[]{:S(2)}) async-start(), calls=%async_computation.4 | async-start | bytes 2359296 | tf_op jit(solution)/shard_map/all_gather | solution.py:61
  225.7 81.1 %all-gather.8.cloned.1.call-start = ((), (), s32[]{:S(2)}) async-start(), calls=%async_computation.5 | async-start | bytes 2359296 | tf_op jit(solution)/shard_map/all_gather | solution.py:61
  228.7 259.3 %reduce-scatter.2.cloned.1.call-start = ((), (), s32[]{:S(2)}) async-start(), calls=%async_computation.6 | async-start | bytes 8650752 | tf_op jit(solution)/shard_map/reduce_scatter | solution.py:68
Sparse Core Ops, SparseCore 0:
  9.8 56.2 all-gather.3
  144.7 78.5 all-reduce.2
  225.8 39.8 all-gather.5
  267.3 39.4 all-gather.7
  389.4 98.5 reduce-scatter.1
where the time goes:
time: 496 us; the launch traced here: 495 us
  waiting for transfers between devices  294 us (59%)
  other arithmetic  61.6 us (12%)
  blocking collectives  59.6 us (12%)
  local copies, waits for them, and re-layouts  43.8 us (9%)
  matrix products  17.9 us (4%)
  between operations  13.4 us (3%)
    reduce_scatter x1, waiting for transfers between devices, body(): lax.psum_scatter(totals.reshape(nblocks, rows_mine, nbasis), 'grid', scat...  98.8 us
    psum x1, waiting for transfers between devices, body(): intersection = lax.psum(intersection_part, 'rows')  77.3 us
    all_gather x2, waiting for transfers between devices, body(): lax.all_gather(potential, 'rows', axis=1, tiled=True)  70.9 us
    scatter-add x2, other arithmetic, body(): totals.at[blocks[:, None], :, blocks[None, :], :]  60.2 us
    all_to_all x1, blocking collectives, copy_for_each(): return lax.all_to_all(copies, axis, split_axis=0, concat_axis=0, tiled=True)  59.6 us
    all_to_all x1, waiting for transfers between devices, copy_for_each(): return lax.all_to_all(copies, axis, split_axis=0, concat_axis=0, tiled=True)  46.5 us
  transfers between devices with their start and end apart: 6, of which 5 were waited for; matrix products, arithmetic and copies ran while one was open for 4% of the time, Pallas kernels for 0%

commit v1 on v0

--- a/solution.py
+++ b/solution.py
@@ -55,10 +55,18 @@
             jnp.dot(x_mine, mixed, preferred_element_type=jnp.float32) * weights[None, :]
         ).astype(jnp.bfloat16)
         potential = potential.reshape(nsig, rows_mine, npoints)
+
+        def recover_slices(along_axis, mine_x, out_dim):
+            wide_out = jax.lax.axis_size(along_axis)
+            everything = jnp.stack([mine_x] * wide_out)
+            then = jax.lax.all_to_all(everything, along_axis, 0, 0)
+            piece_now = jnp.concatenate(then, axis=out_dim)
+            return piece_now
+
         block_k = jnp.einsum(
             "mp,tkp->mtk",
             x_mine,
-            lax.all_gather(potential, "rows", axis=1, tiled=True),
+            recover_slices("rows", potential, 1),
             preferred_element_type=jnp.float32,
         )
         block_k = block_k.reshape(nsig, rows_mine, nsig, block_size)

time: 496 us -> 520 us (1.048)
  waiting for transfers between devices: 294 us -> 304 us
  starting transfers between devices: 4.08 us -> 13 us
  local copies, waits for them, and re-layouts: 43.8 us -> 52 us
    all_to_all x0 -> x2, waiting for transfers between devices: none -> 82.8 us  [recover_slices(): then = jax.lax.all_to_all(everything, along_axis, 0, 0)]
    all_gather x2 -> x0, waiting for transfers between devices: 70.9 us -> none  [body(): lax.all_gather(potential, 'rows', axis=1, tiled=True)]
    all_to_all x0 -> x2, starting transfers between devices: none -> 9.02 us  [recover_slices(): then = jax.lax.all_to_all(everything, along_axis, 0, 0)]
where the time goes in v1:
time: 520 us; the launch traced here: 518 us
  waiting for transfers between devices  304 us (58%)
  other arithmetic  62.6 us (12%)
  blocking collectives  59.6 us (11%)
  local copies, waits for them, and re-layouts  52 us (10%)
  matrix products  14.1 us (3%)
  between operations  13.4 us (3%)
  starting transfers between devices  13 us (2%)
    reduce_scatter x1, waiting for transfers between devices, body(): lax.psum_scatter(totals.reshape(nblocks, rows_mine, nbasis), 'grid', scat...  96.4 us
    all_to_all x2, waiting for transfers between devices, recover_slices(): then = jax.lax.all_to_all(everything, along_axis, 0, 0)  82.8 us
    psum x1, waiting for transfers between devices, body(): intersection = lax.psum(intersection_part, 'rows')  77.3 us
    scatter-add x2, other arithmetic, body(): totals.at[blocks[:, None], :, blocks[None, :], :]  60.2 us
    all_to_all x1, blocking collectives, copy_for_each(): return lax.all_to_all(copies, axis, split_axis=0, concat_axis=0, tiled=True)  59.6 us
    all_to_all x1, waiting for transfers between devices, copy_for_each(): return lax.all_to_all(copies, axis, split_axis=0, concat_axis=0, tiled=True)  46.5 us
  transfers between devices with their start and end apart: 6, of which 5 were waited for; matrix products, arithmetic and copies ran while one was open for 4% of the time, Pallas kernels for 0%

profile of v1, /device:TPU:2, one launch (start us, length us, event | category | flops | bytes accessed | tf_op | source)
XLA Modules:
  0.0 518.3 jit_solution(15890061425346790377)
XLA Ops:
  6.5 0.0 all-gather.2.cloned.1.call-start
  6.5 0.7 all-gather.2.cloned.1.call-update
  7.3 1.2 slice_bitcast_fusion
  8.4 0.0 copy-start
  8.4 0.3 broadcast_in_dim.59
  8.7 59.6 %all_to_all.20 = bf16[8,16,16,512]{3,2,1,0:T(8,128)(2,1)} all-to-all(bf16[8,16,16,512]{3,2,1,0:T(8,128)(2,1)S(1)} %broadcast_in_dim.59), channel_id=1, replica_groups=mesh['grid'=32,'rows'=8] {'rows'}, dimensions={0} | all-to-all | bytes 4194304 | tf_op jit(solution)/shard_map/all_to_all | solution.py:9
  68.3 1.6 broadcast_in_dim.55
  69.9 0.0 copy-start.5
  69.9 3.7 all-to-all-start
  73.6 0.0 all-reduce.3.cloned.1.call-start
  73.7 0.0 copy-done.5
  73.7 3.2 copy.37
  76.9 46.5 %all-to-all-done = bf16[8,16,16,512]{3,2,1,0:T(8,128)(2,1)S(1)} async-done(((bf16[8,16,16,512]{3,2,1,0:T(8,128)(2,1)}), bf16[8,16,16,512]{3,2,1,0:T(8,128)(2,1)S(1)}, u32[]{:S(2)}, u32[]{:S(2)}) %all-to-all-start) | async-done | bytes 2097184 | tf_op jit(solution)/shard_map/all_to_all | solution.py:9
  123.4 1.6 copy.31
  125.0 0.0 all-gather.2.cloned.1.call-done
  125.0 2.9 gather_fusion.2
  127.8 0.3 broadcast_select_fusion
  128.1 0.5 copy.46
  128.6 0.8 copy.36
  129.4 1.7 gather_fusion.3
  131.2 2.9 gather_fusion
  134.0 0.3 broadcast_select_fusion.1
  134.3 0.5 copy.45
  134.8 0.8 copy.30
  135.6 1.7 gather_fusion.1
  137.3 4.1 convolution_bitcast_fusion.2
  141.4 0.0 copy-done.2
  141.4 3.3 convolution_bitcast_fusion.3
  144.7 0.0 all-reduce.3.cloned.1.call-update
  144.7 0.7 copy-done.3
  145.4 0.4 multiply_reduce_fusion.1
  145.8 0.3 copy.29
  146.1 0.0 copy-done.4
  146.1 77.3 %all-reduce.3.cloned.1.call-done = (f32[512,512]{0,1:T(8,128)}, f32[512,512]{0,1:T(8,128)}) async-done(((f32[512,512]{0,1:T(8,128)}, f32[512,512]{0,1:T(8,128)}), (f32[512,512]{0,1:T(8,128)}, f32[512,512]{0,1:T(8,128)})) %all-reduce.3.cloned.1.call-update) | async-done | bytes 2097168 | tf_op jit(solution)/shard_map/psum | solution.py:48
  223.5 0.0 copy-done
  223.5 1.6 fusion
  225.1 1.6 stack.6
  226.7 4.7 all-to-all-start.1
  231.4 1.4 multiply_reduce_fusion
  232.7 1.6 copy.35
  234.3 2.3 fusion.1
  236.6 41.6 %all-to-all-done.1 = bf16[8,16,16,512]{3,2,1,0:T(8,128)(2,1)S(1)} async-done(((bf16[8,16,16,512]{3,2,1,0:T(8,128)(2,1)}), bf16[8,16,16,512]{3,2,1,0:T(8,128)(2,1)S(1)}, u32[]{:S(2)}, u32[]{:S(2)}) %all-to-all-start.1) | async-done | bytes 2097184 | tf_op jit(solution)/shard_map/all_to_all | solution.py:62
  278.2 2.5 stack.7
  280.8 4.3 all-to-all-start.3
  285.1 0.2 reduce-scatter.2.cloned.1.call-start
  285.4 0.1 or_select_fusion
  285.5 0.1 reshape.152
  285.6 0.1 reshape.158
  285.6 0.2 copy.32
  285.9 0.7 copy-done.1
  286.6 0.7 convolution_bitcast_fusion.1
  287.3 2.0 copy.33
  289.3 2.3 copy.34
  291.6 41.2 %all-to-all-done.3 = bf16[8,16,16,512]{3,2,1,0:T(8,128)(2,1)} async-done(((bf16[8,16,16,512]{3,2,1,0:T(8,128)(2,1)}), bf16[8,16,16,512]{3,2,1,0:T(8,128)(2,1)}, u32[]{:S(2)}, u32[]{:S(2)}) %all-to-all-start.3) | async-done | bytes 2097184 | tf_op jit(solution)/shard_map/all_to_all | solution.py:62
  332.7 1.8 copy.38
  334.5 2.1 convolution_bitcast_fusion
  336.6 3.1 copy.39
  339.7 3.6 copy.40
  343.3 4.2 broadcast_in_dim.51
  347.5 28.4 %scatter_fusion = f32[32,16,32,128]{3,1,2,0:T(8,128)} fusion(f32[32,16,32,128]{3,1,2,0:T(8,128)} %broadcast_in_dim.51, s32[256]{0:T(256)S(1)} %reshape.152, f32[256,16,128]{2,1,0:T(8,128)S(1)} %bitcast.111), kind=kCustom, calls=%fused_computation.4 | custom fusion | flops 524288 | bytes 6293504 | tf_op jit(solution)/shard_map/scatter-add | solution.py:73
  375.9 31.8 %scatter_fusion.1 = f32[32,16,32,128]{3,1,2,0:T(8,128)} fusion(f32[32,16,32,128]{3,1,2,0:T(8,128)} %scatter_fusion, s32[256]{0:T(256)S(1)} %reshape.158, f32[256,16,128]{2,1,0:T(8,128)} %bitcast.112), kind=kCustom, calls=%fused_computation.5 | custom fusion | flops 524288 | bytes 6293504 | tf_op jit(solution)/shard_map/scatter-add | solution.py:73
  407.7 7.8 %copy_bitcast_fusion = f32[32,16,4096]{2,1,0:T(8,128)} fusion(f32[32,16,32,128]{3,1,2,0:T(8,128)} %scatter_fusion.1), kind=kLoop, calls=%fused_computation.6 | loop fusion | bytes 16777216 | tf_op jit(solution)/shard_map/reshape | solution.py:77
  415.4 0.0 reduce-scatter.2.cloned.1.call-update
  415.4 96.4 %reduce-scatter.2.cloned.1.call-done = f32[32,16,128]{2,1,0:T(8,128)} async-done(((f32[32,16,4096]{2,1,0:T(8,128)}), f32[32,16,128]{2,1,0:T(8,128)}) %reduce-scatter.2.cloned.1.call-update) | async-done | bytes 262160 | tf_op jit(solution)/shard_map/reduce_scatter | solution.py:76
  (15 shorter events, 0.1 us)
Async XLA Ops:
  6.5 118.4 %all-gather.2.cloned.1.call-start = ((), (), s32[]{:S(2)}) async-start(), calls=%async_computation.5 | async-start | bytes 4325376 | tf_op jit(solution)/shard_map/all_gather | solution.py:30
  8.4 215.1 %copy-start = (bf16[1,16,16,512]{3,2,1,0:T(8,128)(2,1)}, bf16[1,16,16,512]{3,2,1,0:T(8,128)(2,1)S(1)}, u32[]{:S(2)}) copy-start(bf16[1,16,16,512]{3,2,1,0:T(8,128)(2,1)S(1)} %get-tuple-element.16) | copy-start | bytes 786436
  69.9 3.8 copy-start.5
  69.9 53.5 %all-to-all-start = ((bf16[8,16,16,512]{3,2,1,0:T(8,128)(2,1)}), bf16[8,16,16,512]{3,2,1,0:T(8,128)(2,1)S(1)}, u32[]{:S(2)}, u32[]{:S(2)}) async-start(bf16[8,16,16,512]{3,2,1,0:T(8,128)(2,1)} %broadcast_in_dim.55), calls=%async_computation | async-start | bytes 4194304 | tf_op jit(solution)/shard_map/all_to_all | solution.py:9
  73.6 149.9 %all-reduce.3.cloned.1.call-start = ((), (), s32[]{:S(2)}) async-start(), calls=%async_computation.7 | async-start | bytes 4194304 | tf_op jit(solution)/shard_map/psum | solution.py:48
  137.3 4.1 copy-start.2
  144.7 0.7 copy-start.3
  145.4 0.7 copy-start.4
  226.7 51.6 %all-to-all-start.1 = ((bf16[8,16,16,512]{3,2,1,0:T(8,128)(2,1)}), bf16[8,16,16,512]{3,2,1,0:T(8,128)(2,1)S(1)}, u32[]{:S(2)}, u32[]{:S(2)}) async-start(bf16[8,16,16,512]{3,2,1,0:T(8,128)(2,1)} %stack.6), calls=%async_computation.1 | async-start | bytes 4194304 | tf_op jit(solution)/shard_map/all_to_all | solution.py:62
  280.8 52.0 %all-to-all-start.3 = ((bf16[8,16,16,512]{3,2,1,0:T(8,128)(2,1)}), bf16[8,16,16,512]{3,2,1,0:T(8,128)(2,1)}, u32[]{:S(2)}, u32[]{:S(2)}) async-start(bf16[8,16,16,512]{3,2,1,0:T(8,128)(2,1)} %stack.7), calls=%async_computation.3 | async-start | bytes 4194304 | tf_op jit(solution)/shard_map/all_to_all | solution.py:62
  285.1 226.7 %reduce-scatter.2.cloned.1.call-start = ((), (), s32[]{:S(2)}) async-start(), calls=%async_computation.6 | async-start | bytes 8650752 | tf_op jit(solution)/shard_map/reduce_scatter | solution.py:76
  285.6 1.0 copy-start.1
Sparse Core Ops, SparseCore 0:
  9.8 56.2 all-gather.1
  144.8 78.6 all-reduce.2
  415.6 96.1 reduce-scatter.1
